TPU v7x, 32 devices: a whole 2x2x4 slice. The times are simulated.
32 devices in a mesh: angle: 8 (over y, x, core), scan: 4 (over z).
Axes of the slice: x: 2, y: 2, z: 4, core: 2. Of those that a mesh axis runs over, the one named last changes fastest.
Arguments:
- object_slices: float32 [2, 3, 256, 512], P(None, None, 'scan', 'angle'), may hold values from -5 to 5
- probe: float32 [2, 128, 128], replicated, may hold values from -6 to 6
- intensities: float32 [8, 4, 2, 128, 128], P('angle', 'scan'), may hold values from 0.5 to 3.5
- row_offsets: int32 [8, 4, 2], P('angle', 'scan'), may hold values from 0 to 64
- column_starts: int32 [8, 4, 2], P('angle', 'scan'), may hold values from 0 to 320
- slice_shifts: int32 [8, 3], P('angle'), may hold values from 0 to 64
- counts: int32 [8, 4], P('angle', 'scan'), may hold values from 1 to 2, as said below
Outputs:
- object_gradient: float32 [2, 3, 256, 512], P(None, None, 'scan', 'angle')
- probe_gradient: float32 [2, 128, 128], replicated
Inputs may be any that keep to these rules, and one draw needn't show every extreme that they name: `counts`: the largest value 2 occurs in every draw.
All inputs are finite; a program needn't handle non-finite values.
Results may differ from a plain program's by a relative error of at most 0.0003.
Values sent between devices are 32-bit elements; how exact they have to be, the bound alone decides.
A program may use at most 64 MiB of HBM per device.

v0:
```python
from functools import partial
import jax
import jax.numpy as jnp
from jax import lax
from jax.sharding import PartitionSpec as P


def padded(cells, sides, width):
    for axis, dim in sides:
        count = lax.axis_size(axis)
        ends = count - 1
        head = lax.slice_in_dim(cells, 0, width, axis=dim)
        tail = lax.slice_in_dim(cells, cells.shape[dim] - width, cells.shape[dim], axis=dim)
        cells = jnp.concatenate(
            [
                lax.ppermute(tail, axis, [(i, (i + 1) % count) for i in range(ends)]),
                cells,
                lax.ppermute(head, axis, [((i + 1) % count, i) for i in range(ends)]),
            ],
            axis=dim,
        )
    return cells


def propagator(size):
    index = jnp.arange(size, dtype=jnp.int32)
    centred = ((index + size // 2) % size - size // 2).astype(jnp.float32)
    radius = centred[:, None] * centred[:, None] + centred[None, :] * centred[None, :]
    phase = 8.0 * jnp.pi * radius / (size * size)
    return (jnp.cos(phase), jnp.sin(phase))


def tables(size):
    index = jnp.arange(size, dtype=jnp.int32)
    turns = index[:, None] * index[None, :] % size
    phase = 2.0 * jnp.pi * turns.astype(jnp.float32) / size
    scale = 1.0 / jnp.sqrt(jnp.float32(size))
    return (jnp.cos(phase) * scale, jnp.sin(phase) * scale)


def matmul(first, second):
    return jnp.dot(
        first, second, precision=lax.Precision.HIGHEST, preferred_element_type=jnp.float32
    )


def transform(real_part, imag_part, cosine, sine, sign):
    left_re = matmul(cosine, real_part) - sign * matmul(sine, imag_part)
    left_im = matmul(cosine, imag_part) + sign * matmul(sine, real_part)
    right_re = matmul(left_re, cosine) - sign * matmul(left_im, sine)
    right_im = matmul(left_im, cosine) + sign * matmul(left_re, sine)
    return (right_re, right_im)


def local_loss(slab, probe, measured, weight, cosine, sine, kern_re, kern_im):
    wave_re, wave_im = (probe[0], probe[1])
    layers = slab.shape[1]
    for k in range(layers):
        object_re, object_im = (slab[0, k], slab[1, k])
        wave_re, wave_im = (
            wave_re * object_re - wave_im * object_im,
            wave_re * object_im + wave_im * object_re,
        )
        if k + 1 < layers:
            freq_re, freq_im = transform(wave_re, wave_im, cosine, sine, -1.0)
            freq_re, freq_im = (
                freq_re * kern_re - freq_im * kern_im,
                freq_re * kern_im + freq_im * kern_re,
            )
            wave_re, wave_im = transform(freq_re, freq_im, cosine, sine, 1.0)
    far_re, far_im = transform(wave_re, wave_im, cosine, sine, -1.0)
    differ = far_re * far_re + far_im * far_im - measured
    return weight * jnp.sum(differ * differ)


def local(object_slices, probe, intensities, row_offsets, column_starts, slice_shifts, counts):
    band = object_slices.shape[2]
    framed = padded(object_slices, (("scan", 2),), band)
    region = lax.all_gather(framed, "angle", axis=3, tiled=True)
    size = probe.shape[1]
    slots = row_offsets.shape[2]
    layers = region.shape[1]
    angles = lax.axis_size("angle")
    cosine, sine = tables(size)
    kern_re, kern_im = propagator(size)
    shifts = slice_shifts[0]
    zero = jnp.zeros((), jnp.int32)

    def visit(slot, carry):
        gradient_region, gradient_probe = carry
        top = row_offsets[0, 0, slot]
        start = column_starts[0, 0, slot]
        slab = jnp.concatenate(
            [
                lax.dynamic_slice(
                    region, (zero, zero + k, top, start + shifts[k]), (2, 1, size, size)
                )
                for k in range(layers)
            ],
            axis=1,
        )
        weight = jnp.where(slot < counts[0, 0], 0.5 / angles, 0.0).astype(jnp.float32)
        measured = intensities[0, 0, slot]
        scorer = partial(
            local_loss,
            measured=measured,
            weight=weight,
            cosine=cosine,
            sine=sine,
            kern_re=kern_re,
            kern_im=kern_im,
        )
        loss, pull = jax.vjp(scorer, slab, probe)
        slab_grad, probe_grad = pull(jnp.ones_like(loss))
        for k in range(layers):
            place = (zero, zero + k, top, start + shifts[k])
            current = lax.dynamic_slice(gradient_region, place, (2, 1, size, size))
            gradient_region = lax.dynamic_update_slice(
                gradient_region, current + slab_grad[:, k : k + 1], place
            )
        return (gradient_region, gradient_probe + probe_grad)

    start_carry = (jnp.zeros(region.shape, jnp.float32), jnp.zeros(probe.shape, jnp.float32))
    gradient_region, gradient_probe = lax.fori_loop(0, slots, visit, start_carry)
    shared = lax.psum_scatter(gradient_region, "angle", scatter_dimension=3, tiled=True)
    edges = jnp.concatenate([shared[:, :, :band], shared[:, :, 2 * band :]], axis=2)
    rimmed = padded(edges, (("scan", 2),), band)
    object_gradient = shared[:, :, band : 2 * band] + rimmed[:, :, :band] + rimmed[:, :, 3 * band :]
    group_total = lax.psum(gradient_probe, "scan")
    probe_gradient = lax.psum(group_total, "angle")
    return (object_gradient, probe_gradient)


def solution(mesh):
    return jax.shard_map(
        local,
        mesh=mesh,
        in_specs=(
            P(None, None, "scan", "angle"),
            P(),
            P("angle", "scan", None, None, None),
            P("angle", "scan", None),
            P("angle", "scan", None),
            P("angle", None),
            P("angle", "scan"),
        ),
        out_specs=(P(None, None, "scan", "angle"), P()),
        check_vma=False,
    )
```

profile of v0, /device:TPU:0, one launch (start us, length us, event | category | flops | bytes accessed | tf_op | source)
XLA Modules:
  0.0 352.9 jit_solution(17662193562692884179)
XLA Ops:
  7.2 1.1 copy.25
  8.3 1.3 collective-permute-start.1
  9.6 5.6 %collective-permute-start = (f32[2,3,64,64]{2,0,1,3:T(2,128)S(1)}, f32[2,3,64,64]{2,0,1,3:T(2,128)S(1)}, u32[]{:S(2)}, u32[]{:S(2)}) collective-permute-start(f32[2,3,64,64]{2,0,1,3:T(2,128)S(1)} %copy.25), channel_id=1, source_target_pairs={{0,1},{1,2},{2,3},{4,5},{5,6},{6,7},{8,9},{9,10},{10,11},{12,13},{... | collective-permute-start | bytes 294920 | tf_op jit(solution)/shard_map/ppermute | solution.py:16
  15.2 2.9 collective-permute-done.1
  18.2 1.2 collective-permute-done
  19.3 1.2 pad_maximum_fusion
  20.7 34.6 %all-gather.2.cloned.1.call-done = f32[2,3,192,512]{2,0,1,3:T(2,128)} async-done(((f32[2,3,192,64]{2,0,1,3:T(2,128)}), f32[2,3,192,512]{2,0,1,3:T(2,128)}) %all-gather.2.cloned.1.call-update) | async-done | bytes 2359312 | tf_op jit(solution)/shard_map/all_gather | solution.py:79
  55.2 5.6 %copy.28 = f32[2,3,192,512]{3,2,1,0:T(8,128)} copy(f32[2,3,192,512]{2,0,1,3:T(2,128)} %all-gather.2.cloned.1.call-done) | data formatting | bytes 4718592
  61.8 137.1 %while.19 = (s32[]{:T(128)}, f32[2,3,192,512]{3,2,1,0:T(8,128)S(1)}, f32[2,128,128]{2,1,0:T(8,128)S(1)}, s32[1,1,2]{2,1,0:T(1,128)S(1)}, s32[1,1,2]{2,1,0:T(1,12...) while((s32[]{:T(128)}, ...), condition=%wide.region_1.2_spmd.clone.clone.clone.clone, body=%wide.region_0.1_spmd.clone.clone.clone.clone.sunk | while | flops 2037301248 | bytes 20128300 | solution.py:124
  69.6 1.1 fusion.857
  74.6 0.8 fusion.868
  75.5 0.8 convolution_add_fusion.36
  76.8 0.8 fusion.866
  77.6 0.8 convolution_subtract_fusion.8
  79.3 1.5 multiply_add_fusion.7
  84.7 0.8 fusion.880
  85.5 1.3 convolution_add_fusion.37
  87.3 0.8 fusion.878
  88.2 0.8 convolution_subtract_fusion.10
  89.9 1.5 multiply_subtract_fusion.3
  99.0 1.5 add_bitcast_fusion.9
  104.8 0.8 fusion.902
  105.6 0.8 convolution_add_fusion.43
  107.2 0.8 convolution_add_fusion.42
  109.5 1.5 add_bitcast_fusion.10
  115.2 0.8 fusion.913
  116.0 0.8 convolution_add_fusion.47
  117.5 0.8 convolution_add_fusion.46
  120.1 1.5 add_bitcast_fusion.11
  121.8 2.3 dynamic_update_slice.36
  124.3 2.3 dynamic_update_slice.37
  126.7 2.3 dynamic_update_slice.38
  137.1 1.1 fusion.857
  142.1 0.8 fusion.868
  142.9 0.8 convolution_add_fusion.36
  144.2 0.8 fusion.866
  145.0 0.8 convolution_subtract_fusion.8
  146.8 1.5 multiply_add_fusion.7
  152.2 0.8 fusion.880
  153.0 1.0 convolution_add_fusion.37
  154.5 0.8 fusion.878
  155.3 0.8 convolution_subtract_fusion.10
  157.0 1.5 multiply_subtract_fusion.3
  166.1 1.5 add_bitcast_fusion.9
  172.0 0.8 fusion.902
  172.7 0.8 convolution_add_fusion.43
  174.3 0.8 convolution_add_fusion.42
  176.7 1.5 add_bitcast_fusion.10
  182.3 0.8 fusion.913
  184.7 0.8 convolution_add_fusion.46
  186.5 0.9 fusion.914
  187.4 1.5 add_bitcast_fusion.11
  189.2 2.3 dynamic_update_slice.36
  191.6 2.3 dynamic_update_slice.37
  194.0 2.3 dynamic_update_slice.38
  199.0 3.4 copy.37
  202.4 6.0 %reshape.42 = f32[512,1152]{1,0:T(8,128)} reshape(f32[512,2,3,192]{3,2,1,0:T(4,128)} %bitcast.367) | data formatting | bytes 4718592
  209.2 41.8 %reduce-scatter.4.cloned.1.call-done = f32[64,1152]{1,0:T(8,128)} async-done(((f32[512,1152]{1,0:T(8,128)}), f32[64,1152]{1,0:T(8,128)}) %reduce-scatter.4.cloned.1.call-update) | async-done | bytes 294928
  250.9 1.3 reshape.43
  252.8 1.3 collective-permute-start.3
  254.1 4.6 %collective-permute-start.2 = (f32[2,3,64,64]{3,2,1,0:T(8,128)S(1)}, f32[2,3,64,64]{3,2,1,0:T(8,128)S(1)}, u32[]{:S(2)}, u32[]{:S(2)}) collective-permute-start(f32[2,3,64,64]{3,2,1,0:T(8,128)S(1)} %copy.40), channel_id=1, source_target_pairs={{0,1},{1,2},{2,3},{4,5},{5,6},{6,7},{8,9},{9,10},{10,11},{12,13},{... | collective-permute-start | bytes 294920 | tf_op jit(solution)/shard_map/ppermute | solution.py:16
  258.6 29.9 %all-reduce.11.cloned.1.call-done = f32[2,128,128]{2,1,0:T(8,128)} async-done(((f32[2,128,128]{2,1,0:T(8,128)}), f32[2,128,128]{2,1,0:T(8,128)}) %all-reduce.11.cloned.1.call-update) | async-done | bytes 131088 | tf_op jit(solution)/shard_map/psum | solution.py:129
  289.4 55.2 %all-reduce.13.cloned.1.call-done = f32[2,128,128]{2,1,0:T(8,128)} async-done(((f32[2,128,128]{2,1,0:T(8,128)}), f32[2,128,128]{2,1,0:T(8,128)}) %all-reduce.13.cloned.1.call-update) | async-done | bytes 131088 | tf_op jit(solution)/shard_map/psum | solution.py:130
  344.6 1.6 copy.56
  (166 shorter events, 69.4 us)
Async XLA Ops:
  7.2 48.1 %all-gather.2.cloned.1.call-start = ((), (), s32[]{:S(2)}) async-start(), calls=%async_computation.1 | async-start | bytes 3538944 | tf_op jit(solution)/shard_map/all_gather | solution.py:79
  8.3 9.9 %collective-permute-start.1 = (f32[2,3,64,64]{2,0,1,3:T(2,128)S(1)}, f32[2,3,64,64]{2,0,1,3:T(2,128)S(1)}, u32[]{:S(2)}, u32[]{:S(2)}) collective-permute-start(f32[2,3,64,64]{2,0,1,3:T(2,128)S(1)} %copy.25), channel_id=1, source_target_pairs={{1,0},{2,1},{3,2},{5,4},{6,5},{7,6},{9,8},{10,9},{11,10},{13,12},{... | collective-permute-start | bytes 294920 | tf_op jit(solution)/shard_map/ppermute | solution.py:18
  9.6 9.7 %collective-permute-start = (f32[2,3,64,64]{2,0,1,3:T(2,128)S(1)}, f32[2,3,64,64]{2,0,1,3:T(2,128)S(1)}, u32[]{:S(2)}, u32[]{:S(2)}) collective-permute-start(f32[2,3,64,64]{2,0,1,3:T(2,128)S(1)} %copy.25), channel_id=1, source_target_pairs={{0,1},{1,2},{2,3},{4,5},{5,6},{6,7},{8,9},{9,10},{10,11},{12,13},{... | collective-permute-start | bytes 294920 | tf_op jit(solution)/shard_map/ppermute | solution.py:16
  20.6 230.3 %reduce-scatter.4.cloned.1.call-start = ((), (), s32[]{:S(2)}) async-start(), calls=%async_computation.4 | async-start | bytes 2654208
  60.8 0.9 copy-start
  60.8 0.9 copy-start.2
  60.8 0.9 copy-start.3
  60.8 0.9 copy-start.4
  60.8 1.0 copy-start.5
  199.0 3.4 copy-start.1
  208.4 80.1 %all-reduce.11.cloned.1.call-start = ((), (), s32[]{:S(2)}) async-start(), calls=%async_computation.2 | async-start | bytes 262144 | tf_op jit(solution)/shard_map/psum | solution.py:129
  209.1 135.5 %all-reduce.13.cloned.1.call-start = ((), (), s32[]{:S(2)}) async-start(), calls=%async_computation.3 | async-start | bytes 262144 | tf_op jit(solution)/shard_map/psum | solution.py:130
  252.8 35.9 %collective-permute-start.3 = (f32[2,3,64,64]{3,2,1,0:T(8,128)S(1)}, f32[2,3,64,64]{3,2,1,0:T(8,128)S(1)}, u32[]{:S(2)}, u32[]{:S(2)}) collective-permute-start(f32[2,3,64,64]{3,2,1,0:T(8,128)S(1)} %copy.41), channel_id=1, source_target_pairs={{1,0},{2,1},{3,2},{5,4},{6,5},{7,6},{9,8},{10,9},{11,10},{13,12},{... | collective-permute-start | bytes 294920 | tf_op jit(solution)/shard_map/ppermute | solution.py:18
  254.1 34.6 %collective-permute-start.2 = (f32[2,3,64,64]{3,2,1,0:T(8,128)S(1)}, f32[2,3,64,64]{3,2,1,0:T(8,128)S(1)}, u32[]{:S(2)}, u32[]{:S(2)}) collective-permute-start(f32[2,3,64,64]{3,2,1,0:T(8,128)S(1)} %copy.40), channel_id=1, source_target_pairs={{0,1},{1,2},{2,3},{4,5},{5,6},{6,7},{8,9},{9,10},{10,11},{12,13},{... | collective-permute-start | bytes 294920 | tf_op jit(solution)/shard_map/ppermute | solution.py:16
Sparse Core Ops, SparseCore 0:
  20.7 34.4 all-gather.1
  208.5 42.3 reduce-scatter.3
  253.8 34.6 all-reduce.10
  291.4 53.1 all-reduce.12
where the time goes:
time: 356 us; the launch traced here: 353 us
  waiting for transfers between devices  166 us (47%)
  matrix products  101 us (28%)
  local copies, waits for them, and re-layouts  36.8 us (10%)
  loops' own time  16.9 us (5%)
  between operations  14.1 us (4%)
  starting transfers between devices  12.9 us (4%)
  other arithmetic  4.94 us (1%)
    dot_general x160, matrix products, matmul(): jnp.dot(first, second, precision=lax.Precision.HIGHEST, preferred_element...  101 us
    psum x1, waiting for transfers between devices, local(): probe_gradient = lax.psum(group_total, 'angle')  55.2 us
    unnamed x5, waiting for transfers between devices  42.5 us
    all_gather x1, waiting for transfers between devices, local(): region = lax.all_gather(framed, 'angle', axis=3, tiled=True)  34.6 us
    psum x1, waiting for transfers between devices, local(): group_total = lax.psum(gradient_probe, 'scan')  29.9 us
    unnamed x21, local copies, waits for them, and re-layouts  20 us
    another operation x1, loops' own time, local(): lax.fori_loop(0, slots, visit, start_carry)  16.9 us
    dynamic_update_slice x6, local copies, waits for them, and re-layouts, visit(): lax.dynamic_update_slice(gradient_region, current + slab_grad[:, k:k + 1]...  13.8 us
  transfers between devices with their start and end apart: 8, of which 6 were waited for; matrix products, arithmetic and copies ran while one was open for 1% of the time, Pallas kernels for 0%

commit v1 on v0

--- a/solution.py
+++ b/solution.py
@@ -126,7 +126,7 @@
     edges = jnp.concatenate([shared[:, :, :band], shared[:, :, 2 * band :]], axis=2)
     rimmed = padded(edges, (("scan", 2),), band)
     object_gradient = shared[:, :, band : 2 * band] + rimmed[:, :, :band] + rimmed[:, :, 3 * band :]
-    group_total = lax.psum(gradient_probe, "scan")
+    group_total = jnp.sum(lax.all_gather(gradient_probe, "scan"), 0)
     probe_gradient = lax.psum(group_total, "angle")
     return (object_gradient, probe_gradient)
 

time: 356 us -> 341 us (0.958)
  waiting for transfers between devices: 166 us -> 134 us
  blocking collectives: 0 us -> 16.9 us
    psum x1 -> x0, waiting for transfers between devices: 29.9 us -> none  [local(): group_total = lax.psum(gradient_probe, 'scan')]
    all_gather x0 -> x1, blocking collectives: none -> 16.9 us  [local(): group_total = jnp.sum(lax.all_gather(gradient_probe, 'scan'), 0)]
    unnamed x5 -> x4, waiting for transfers between devices: 42.5 us -> 42.6 us
    unnamed x21 -> x19, local copies, waits for them, and re-layouts: 20 us -> 20 us
  transfers between devices with their start and end apart: 8 -> 7, of which waited for: 6 -> 5; matrix products, arithmetic and copies ran while one was open for 1% -> 0% of each run, Pallas kernels for 0% -> 0%
where the time goes in v1:
time: 341 us; the launch traced here: 338 us
  waiting for transfers between devices  134 us (39%)
  matrix products  101 us (30%)
  local copies, waits for them, and re-layouts  36.7 us (11%)
  blocking collectives  16.9 us (5%)
  loops' own time  16.4 us (5%)
  between operations  14.1 us (4%)
  starting transfers between devices  12.9 us (4%)
  other arithmetic  5.66 us (2%)
    dot_general x160, matrix products, matmul(): jnp.dot(first, second, precision=lax.Precision.HIGHEST, preferred_element...  101 us
    psum x1, waiting for transfers between devices, local(): probe_gradient = lax.psum(group_total, 'angle')  53.2 us
    unnamed x4, waiting for transfers between devices  42.6 us
    all_gather x1, waiting for transfers between devices, local(): region = lax.all_gather(framed, 'angle', axis=3, tiled=True)  34.6 us
    unnamed x19, local copies, waits for them, and re-layouts  20 us
    all_gather x1, blocking collectives, local(): group_total = jnp.sum(lax.all_gather(gradient_probe, 'scan'), 0)  16.9 us
    another operation x1, loops' own time, local(): lax.fori_loop(0, slots, visit, start_carry)  16.4 us
    dynamic_update_slice x6, local copies, waits for them, and re-layouts, visit(): lax.dynamic_update_slice(gradient_region, current + slab_grad[:, k:k + 1]...  13.8 us
  transfers between devices with their start and end apart: 7, of which 5 were waited for; matrix products, arithmetic and copies ran while one was open for 0% of the time, Pallas kernels for 0%

profile of v1, /device:TPU:0, one launch (start us, length us, event | category | flops | bytes accessed | tf_op | source)
XLA Modules:
  0.0 338.0 jit_solution(12044905494210382741)
XLA Ops:
  7.2 1.1 copy.25
  8.3 1.3 collective-permute-start.1
  9.6 5.6 %collective-permute-start = (f32[2,3,64,64]{2,0,1,3:T(2,128)S(1)}, f32[2,3,64,64]{2,0,1,3:T(2,128)S(1)}, u32[]{:S(2)}, u32[]{:S(2)}) collective-permute-start(f32[2,3,64,64]{2,0,1,3:T(2,128)S(1)} %copy.25), channel_id=1, source_target_pairs={{0,1},{1,2},{2,3},{4,5},{5,6},{6,7},{8,9},{9,10},{10,11},{12,13},{... | collective-permute-start | bytes 294920 | tf_op jit(solution)/shard_map/ppermute | solution.py:16
  15.2 2.9 collective-permute-done.1
  18.2 1.2 collective-permute-done
  19.3 1.2 pad_maximum_fusion
  20.7 34.6 %all-gather.3.cloned.1.call-done = f32[2,3,192,512]{2,0,1,3:T(2,128)} async-done(((f32[2,3,192,64]{2,0,1,3:T(2,128)}), f32[2,3,192,512]{2,0,1,3:T(2,128)}) %all-gather.3.cloned.1.call-update) | async-done | bytes 2359312 | tf_op jit(solution)/shard_map/all_gather | solution.py:79
  55.3 5.5 %copy.28 = f32[2,3,192,512]{3,2,1,0:T(8,128)} copy(f32[2,3,192,512]{2,0,1,3:T(2,128)} %all-gather.3.cloned.1.call-done) | data formatting | bytes 4718592
  61.8 136.5 %while.19 = (s32[]{:T(128)}, f32[2,3,192,512]{3,2,1,0:T(8,128)S(1)}, f32[2,128,128]{2,1,0:T(8,128)S(1)}, s32[1,1,2]{2,1,0:T(1,128)S(1)}, s32[1,1,2]{2,1,0:T(1,12...) while((s32[]{:T(128)}, ...), condition=%wide.region_1.2_spmd.clone.clone.clone.clone, body=%wide.region_0.1_spmd.clone.clone.clone.clone.sunk | while | flops 2037301248 | bytes 20128300 | solution.py:124
  69.3 1.1 fusion.857
  74.3 0.8 fusion.868
  75.1 0.8 convolution_add_fusion.36
  76.4 0.8 fusion.866
  77.2 0.8 convolution_subtract_fusion.8
  79.0 1.5 multiply_add_fusion.7
  84.4 0.8 fusion.880
  85.2 1.3 convolution_add_fusion.37
  87.0 0.8 fusion.878
  87.8 0.8 convolution_subtract_fusion.10
  89.6 1.5 multiply_subtract_fusion.3
  98.6 1.5 add_bitcast_fusion.9
  104.5 0.8 fusion.902
  105.3 0.8 convolution_add_fusion.43
  106.8 0.8 convolution_add_fusion.42
  109.2 1.5 add_bitcast_fusion.10
  114.9 0.8 fusion.913
  115.6 0.8 convolution_add_fusion.47
  117.2 0.8 convolution_add_fusion.46
  119.8 1.5 add_bitcast_fusion.11
  121.5 2.3 dynamic_update_slice.36
  123.9 2.3 dynamic_update_slice.37
  126.4 2.3 dynamic_update_slice.38
  136.4 1.1 fusion.857
  141.4 0.8 fusion.868
  142.3 0.8 convolution_add_fusion.36
  143.5 0.8 fusion.866
  144.4 0.8 convolution_subtract_fusion.8
  146.1 1.5 multiply_add_fusion.7
  151.5 0.8 fusion.880
  152.3 1.0 convolution_add_fusion.37
  153.8 0.8 fusion.878
  154.6 0.8 convolution_subtract_fusion.10
  156.4 1.5 multiply_subtract_fusion.3
  165.4 1.5 add_bitcast_fusion.9
  171.3 0.8 fusion.902
  172.1 0.8 convolution_add_fusion.43
  173.6 0.8 convolution_add_fusion.42
  176.0 1.5 add_bitcast_fusion.10
  181.7 0.8 fusion.913
  184.0 0.8 convolution_add_fusion.46
  185.8 0.9 fusion.914
  186.8 1.5 add_bitcast_fusion.11
  188.5 2.3 dynamic_update_slice.36
  190.9 2.3 dynamic_update_slice.37
  193.3 2.3 dynamic_update_slice.38
  198.3 3.4 %copy.37 = f32[2,3,192,512]{2,1,0,3:T(4,128)} copy(f32[2,3,192,512]{3,2,1,0:T(8,128)S(1)} %get-tuple-element.508) | data formatting | bytes 4718592
  201.8 6.0 %reshape.43 = f32[512,1152]{1,0:T(8,128)} reshape(f32[512,2,3,192]{3,2,1,0:T(4,128)} %bitcast.368) | data formatting | bytes 4718592
  207.8 42.5 %reduce-scatter.4.cloned.1.call-done = f32[64,1152]{1,0:T(8,128)} async-done(((f32[512,1152]{1,0:T(8,128)}), f32[64,1152]{1,0:T(8,128)}) %reduce-scatter.4.cloned.1.call-update) | async-done | bytes 294928
  250.3 1.3 reshape.44
  252.2 1.3 collective-permute-start.3
  253.5 4.6 %collective-permute-start.2 = (f32[2,3,64,64]{3,2,1,0:T(8,128)S(1)}, f32[2,3,64,64]{3,2,1,0:T(8,128)S(1)}, u32[]{:S(2)}, u32[]{:S(2)}) collective-permute-start(f32[2,3,64,64]{3,2,1,0:T(8,128)S(1)} %copy.40), channel_id=1, source_target_pairs={{0,1},{1,2},{2,3},{4,5},{5,6},{6,7},{8,9},{9,10},{10,11},{12,13},{... | collective-permute-start | bytes 294920 | tf_op jit(solution)/shard_map/ppermute | solution.py:16
  258.0 16.9 %all-gather = f32[8,128,128]{2,1,0:T(8,128)S(1)} all-gather(f32[2,128,128]{2,1,0:T(8,128)S(1)} %get-tuple-element.509), channel_id=2, replica_groups=mesh['angle'=8,'scan'=4] {'scan'}, dimensions={0}, use_global_device_ids=true | all-gather | bytes 655360 | tf_op jit(solution)/shard_map/all_gather | solution.py:129
  276.5 53.2 %all-reduce.10.cloned.1.call-done = f32[2,128,128]{2,1,0:T(8,128)} async-done(((f32[2,128,128]{2,1,0:T(8,128)}), f32[2,128,128]{2,1,0:T(8,128)}) %all-reduce.10.cloned.1.call-update) | async-done | bytes 131088 | tf_op jit(solution)/shard_map/psum | solution.py:130
  329.7 1.6 copy.55
  (163 shorter events, 69.2 us)
Async XLA Ops:
  7.2 48.1 %all-gather.3.cloned.1.call-start = ((), (), s32[]{:S(2)}) async-start(), calls=%async_computation.1 | async-start | bytes 3538944 | tf_op jit(solution)/shard_map/all_gather | solution.py:79
  8.3 9.9 %collective-permute-start.1 = (f32[2,3,64,64]{2,0,1,3:T(2,128)S(1)}, f32[2,3,64,64]{2,0,1,3:T(2,128)S(1)}, u32[]{:S(2)}, u32[]{:S(2)}) collective-permute-start(f32[2,3,64,64]{2,0,1,3:T(2,128)S(1)} %copy.25), channel_id=1, source_target_pairs={{1,0},{2,1},{3,2},{5,4},{6,5},{7,6},{9,8},{10,9},{11,10},{13,12},{... | collective-permute-start | bytes 294920 | tf_op jit(solution)/shard_map/ppermute | solution.py:18
  9.6 9.7 %collective-permute-start = (f32[2,3,64,64]{2,0,1,3:T(2,128)S(1)}, f32[2,3,64,64]{2,0,1,3:T(2,128)S(1)}, u32[]{:S(2)}, u32[]{:S(2)}) collective-permute-start(f32[2,3,64,64]{2,0,1,3:T(2,128)S(1)} %copy.25), channel_id=1, source_target_pairs={{0,1},{1,2},{2,3},{4,5},{5,6},{6,7},{8,9},{9,10},{10,11},{12,13},{... | collective-permute-start | bytes 294920 | tf_op jit(solution)/shard_map/ppermute | solution.py:16
  20.6 229.7 %reduce-scatter.4.cloned.1.call-start = ((), (), s32[]{:S(2)}) async-start(), calls=%async_computation.3 | async-start | bytes 2654208
  60.8 0.9 copy-start
  60.8 0.9 copy-start.1
  60.8 0.9 copy-start.2
  60.8 0.9 copy-start.3
  60.8 1.0 copy-start.4
  207.8 121.9 %all-reduce.10.cloned.1.call-start = ((), (), s32[]{:S(2)}) async-start(), calls=%async_computation.2 | async-start | bytes 262144 | tf_op jit(solution)/shard_map/psum | solution.py:130
  252.2 23.6 %collective-permute-start.3 = (f32[2,3,64,64]{3,2,1,0:T(8,128)S(1)}, f32[2,3,64,64]{3,2,1,0:T(8,128)S(1)}, u32[]{:S(2)}, u32[]{:S(2)}) collective-permute-start(f32[2,3,64,64]{3,2,1,0:T(8,128)S(1)} %copy.41), channel_id=1, source_target_pairs={{1,0},{2,1},{3,2},{5,4},{6,5},{7,6},{9,8},{10,9},{11,10},{13,12},{... | collective-permute-start | bytes 294920 | tf_op jit(solution)/shard_map/ppermute | solution.py:18
  253.5 22.3 %collective-permute-start.2 = (f32[2,3,64,64]{3,2,1,0:T(8,128)S(1)}, f32[2,3,64,64]{3,2,1,0:T(8,128)S(1)}, u32[]{:S(2)}, u32[]{:S(2)}) collective-permute-start(f32[2,3,64,64]{3,2,1,0:T(8,128)S(1)} %copy.40), channel_id=1, source_target_pairs={{0,1},{1,2},{2,3},{4,5},{5,6},{6,7},{8,9},{9,10},{10,11},{12,13},{... | collective-permute-start | bytes 294920 | tf_op jit(solution)/shard_map/ppermute | solution.py:16
Sparse Core Ops, SparseCore 0:
  20.7 34.4 all-gather.2
  207.9 42.3 reduce-scatter.3
  275.7 53.8 all-reduce.9
